TPU v7x, 32 devices: a whole 2x2x4 slice. The times are simulated.
32 devices in a mesh: grp: 4 (over z), kv: 4 (over y, x), tp: 2 (over core).
Axes of the slice: x: 2, y: 2, z: 4, core: 2. Of those that a mesh axis runs over, the one named last changes fastest.
Arguments:
- hidden_states: bfloat16 [512, 4096], P('grp', 'kv'), may hold values from -6 to 6
- attn_gain: float32 [4096], P('kv'), may hold values from 0.25 to 1.75
- mlp_gain: float32 [4096], replicated, may hold values from 0.25 to 1.75
- w_query: bfloat16 [4096, 4096], P('kv', 'tp'), may hold values from -0.09375 to 0.09375
- w_out: bfloat16 [32, 128, 4096], P('tp', 'kv'), may hold values from -1 to 1
- w_gate: bfloat16 [4096, 14336], P(None, ('kv', 'tp')), may hold values from -0.09375 to 0.09375
- w_up: bfloat16 [4096, 14336], P(None, ('kv', 'tp')), may hold values from -0.09375 to 0.09375
- w_down: bfloat16 [14336, 4096], P(('kv', 'tp')), may hold values from -0.046875 to 0.046875
- kv_pool: bfloat16 [256, 2, 128, 1024], P(('grp', 'kv'), None, None, 'tp'), may hold values from -110 to 110
- resident_cache: bfloat16 [4, 32, 2, 128, 1024], P('grp', 'kv', None, None, 'tp'), may hold values from -110 to 110
- resident_slot: int32 [4, 32], P('grp', 'kv'), may hold values from 0 to 127
- resident_len: int32 [4, 32], P('grp', 'kv'), may hold values from 1 to 128
- new_owner: int32 [4, 64], replicated, may hold values from 0 to 15, as said below
- new_local: int32 [4, 64], replicated, may hold values from 0 to 15
- new_slot: int32 [4, 64], P('grp', 'kv'), may hold values from 0 to 127
- new_len: int32 [4, 64], P('grp', 'kv'), may hold values from 1 to 128
- token_kv: bfloat16 [512, 2, 1024], P('grp', None, 'tp'), may hold values from -6 to 6
Outputs:
- mixed: bfloat16 [512, 4096], P(('grp', 'kv', 'tp'))
- new_cache: bfloat16 [4, 64, 2, 128, 1024], P('grp', 'kv', None, None, 'tp')
Inputs may be any that keep to these rules, and one draw needn't show every extreme that they name: New page c of group g is kept by the device of kv index c // 16 of group g and comes from the device whose index along grp+kv is new_owner[g, c]; every decode device receives exactly 4 new pages from the owners of each grp index; no owner sends more than 4 pages to the devices of one kv index over all groups, so at most 4 to one device; every owner sends each of its 16 pages exactly once.
All inputs are finite; a program needn't handle non-finite values.
Results may differ from a plain program's by a relative error of at most 0.018.
Values may be sent and summed in bfloat16 or wider, within the bound.
No kernel may reach another device: no remote copies, remote signals or barrier semaphores. Data moves between devices by JAX's collectives and lax.ppermute only.
A program may use at most 128 MiB of HBM per device.

v0:
```python
import jax
import jax.numpy as jnp
from jax import lax
from jax.sharding import PartitionSpec as P

D = 4096
HEADS = 32
KV_HEADS = 8
HEAD_DIM = 128
NPR = 4
neg_fill = -1e30
norm_eps = 1e-05


def combined_all(part, axis, combine):
    gathered = jax.tree.map(lambda a: lax.all_gather(a, axis), part)

    def take(source):
        return jax.tree.map(lambda a: lax.dynamic_index_in_dim(a, source, 0, False), gathered)

    return lax.fori_loop(
        1, lax.axis_size(axis), lambda source, state: combine(state, take(source)), take(0)
    )


def combine(earlier, later):
    top_a, sum_a, acc_a = earlier
    top_b, sum_b, acc_b = later
    top = jnp.maximum(top_a, top_b)
    fade_a = jnp.exp(top_a - top)
    fade_b = jnp.exp(top_b - top)
    return (
        top,
        sum_a * fade_a + sum_b * fade_b,
        acc_a * fade_a[..., None] + acc_b * fade_b[..., None],
    )


def nth_match(table, wanted, places):
    matched = (table == wanted).astype(jnp.int32)
    ranking = jnp.cumsum(matched, axis=1) - 1
    return (matched[:, None, :] == 1) & (ranking[:, None, :] == places[None, :, None])


def move_pages(kv_pool, new_owner, new_local):
    groups = lax.axis_size("grp")
    ranks = lax.axis_size("kv")
    per_dev = new_owner.shape[1] // ranks
    cap = groups * NPR // ranks
    grp_rank = lax.axis_index("grp")
    kv_rank = lax.axis_index("kv")
    owners = new_owner.reshape(groups * ranks, per_dev)
    myself = grp_rank * ranks + kv_rank
    places = jnp.arange(cap, dtype=jnp.int32)
    mine = lax.dynamic_index_in_dim(owners, myself, 0, keepdims=False)
    order = jnp.arange(per_dev, dtype=jnp.int32)
    by_col = (
        new_owner.reshape(groups, ranks, per_dev)
        .transpose(1, 0, 2)
        .reshape(ranks, groups * per_dev)
    )
    local_col = (
        new_local.reshape(groups, ranks, per_dev)
        .transpose(1, 0, 2)
        .reshape(ranks, groups * per_dev)
    )
    select = nth_match(by_col, myself, places)
    picked = jnp.sum(jnp.where(select, local_col[:, None, :], 0), axis=2)
    outgoing = jnp.take(kv_pool, picked.reshape(-1), axis=0)
    received = lax.all_to_all(outgoing, "kv", split_axis=0, concat_axis=0, tiled=True)
    row_here = lax.dynamic_index_in_dim(by_col, kv_rank, 0, keepdims=False)
    sources = grp_rank * ranks + jnp.arange(ranks, dtype=jnp.int32)
    hits = nth_match(
        jnp.broadcast_to(row_here[None, :], (ranks, row_here.shape[0])), sources[:, None], places
    )
    spots = jnp.arange(row_here.shape[0], dtype=jnp.int32)
    where_f = jnp.sum(jnp.where(hits, spots[None, None, :], 0), axis=2).reshape(-1)
    dest_grp = where_f // per_dev
    dest_pos = where_f % per_dev
    same = (dest_grp[:, None] == dest_grp[None, :]) & (dest_pos[:, None] < dest_pos[None, :])
    rank_in = jnp.sum(same.astype(jnp.int32), axis=0)
    target = dest_grp * NPR + rank_in
    items = jnp.arange(target.shape[0], dtype=jnp.int32)
    inverse = jnp.sum(jnp.where(target[None, :] == items[:, None], items[None, :], 0), axis=1)
    sorted_pages = jnp.take(received, inverse, axis=0)
    arrived = lax.all_to_all(sorted_pages, "grp", split_axis=0, concat_axis=0, tiled=True)
    src_grp = mine // ranks
    earlier = (src_grp[:, None] == src_grp[None, :]) & (order[:, None] < order[None, :])
    before = jnp.sum(earlier.astype(jnp.int32), axis=0)
    return jnp.take(arrived, src_grp * NPR + before, axis=0)


def local_partials(query, resident, arrived, res_slot, res_len, arr_slot, arr_len, token_kv, first):
    pages = jnp.concatenate([resident, arrived], axis=0)
    owner_slot = jnp.concatenate([res_slot, arr_slot])
    filled = jnp.concatenate([res_len, arr_len])
    count = pages.shape[0]
    tokens = pages.shape[2]
    kv_here = pages.shape[3] // HEAD_DIM
    slots = query.shape[0]
    ratio = HEADS // KV_HEADS
    keys = pages[:, 0].astype(jnp.float32).reshape(count, tokens, kv_here, HEAD_DIM)
    values = pages[:, 1].astype(jnp.float32).reshape(count, tokens, kv_here, HEAD_DIM)
    grouped = query.reshape(slots, kv_here, ratio, HEAD_DIM)
    picked = jnp.take(grouped, owner_slot, axis=0)
    scores = jnp.einsum("ikgd,itkd->ikgt", picked, keys, precision=lax.Precision.HIGHEST)
    usable = (jnp.arange(tokens, dtype=jnp.int32)[None, :] < filled[:, None])[:, None, None, :]
    scores = jnp.where(usable, scores, neg_fill)
    page_top = jnp.max(scores, axis=3)
    member = owner_slot[None, :] == jnp.arange(slots, dtype=jnp.int32)[:, None]
    slot_top = jnp.max(jnp.where(member[:, :, None, None], page_top[None], neg_fill), axis=1)
    own_keys = token_kv[:, 0].astype(jnp.float32).reshape(slots, kv_here, HEAD_DIM)
    own_values = token_kv[:, 1].astype(jnp.float32).reshape(slots, kv_here, HEAD_DIM)
    own_score = jnp.einsum("skgd,skd->skg", grouped, own_keys, precision=lax.Precision.HIGHEST)
    own_score = jnp.where(first, own_score, neg_fill)
    slot_top = jnp.maximum(slot_top, own_score)
    reach = jnp.take(slot_top, owner_slot, axis=0)
    weights = jnp.where(usable, jnp.exp(scores - reach[..., None]), 0.0)
    page_sum = jnp.sum(weights, axis=3)
    page_acc = jnp.einsum("ikgt,itkd->ikgd", weights, values, precision=lax.Precision.HIGHEST)
    own_weight = jnp.where(first, jnp.exp(own_score - slot_top), 0.0)
    member_f = member.astype(jnp.float32)
    total = jnp.dot(member_f, page_sum.reshape(count, -1), precision=lax.Precision.HIGHEST)
    total = total + own_weight.reshape(slots, -1)
    weighted = jnp.dot(member_f, page_acc.reshape(count, -1), precision=lax.Precision.HIGHEST)
    weighted = (
        weighted.reshape(slots, kv_here, ratio, HEAD_DIM)
        + own_weight[..., None] * own_values[:, :, None, :]
    )
    return (slot_top.reshape(slots, -1), total, weighted.reshape(slots, kv_here * ratio, HEAD_DIM))


def per_device(
    hidden_states,
    attn_gain,
    mlp_gain,
    w_query,
    w_out,
    w_gate,
    w_up,
    w_down,
    kv_pool,
    resident_cache,
    resident_slot,
    resident_len,
    new_owner,
    new_local,
    new_slot,
    new_len,
    token_kv,
):
    ranks = lax.axis_size("kv")
    pairs = lax.axis_size("tp")
    kv_rank = lax.axis_index("kv")
    tp_rank = lax.axis_index("tp")
    features = hidden_states.astype(jnp.float32)
    partial_query = jnp.dot(
        (features * attn_gain).astype(jnp.bfloat16), w_query, preferred_element_type=jnp.float32
    )
    squares = jnp.sum(features * features, axis=1)
    partial_query, squares = lax.psum((partial_query, squares), "kv")
    attn_scale = lax.rsqrt(squares / D + norm_eps)
    query = partial_query * attn_scale[:, None] * HEAD_DIM ** (-0.5)
    new_pages = move_pages(kv_pool, new_owner, new_local)
    top, total, weighted = local_partials(
        query,
        resident_cache[0],
        new_pages,
        resident_slot[0],
        resident_len[0],
        new_slot[0],
        new_len[0],
        token_kv,
        kv_rank == 0,
    )
    top, total, weighted = combined_all((top, total, weighted), "kv", combine)
    attn = (weighted / total[..., None]).astype(jnp.bfloat16)
    slots = attn.shape[0]
    heads_here = attn.shape[1]
    span = HEAD_DIM // ranks
    piece = lax.dynamic_slice_in_dim(attn, kv_rank * span, span, 2)
    branch = jnp.dot(
        piece.reshape(slots, heads_here * span),
        w_out.reshape(heads_here * span, w_out.shape[2]),
        preferred_element_type=jnp.float32,
    )
    width_here = hidden_states.shape[1]
    laid = branch.reshape(slots, ranks, width_here)
    spot = (jnp.arange(ranks, dtype=jnp.int32) == kv_rank) & (tp_rank == 0)
    laid = laid + jnp.where(spot[None, :, None], features[:, None, :], 0.0)
    resid = lax.psum(laid.reshape(slots, ranks * width_here).astype(jnp.bfloat16), ("kv", "tp"))
    resid_f = resid.astype(jnp.float32)
    mlp_scale = lax.rsqrt(jnp.sum(resid_f * resid_f, axis=1) / D + norm_eps)
    normed_mlp = (resid_f * mlp_gain).astype(jnp.bfloat16)
    gate = jnp.dot(normed_mlp, w_gate, preferred_element_type=jnp.float32) * mlp_scale[:, None]
    upward = jnp.dot(normed_mlp, w_up, preferred_element_type=jnp.float32) * mlp_scale[:, None]
    hidden_units = (jax.nn.silu(gate) * upward).astype(jnp.bfloat16)
    row_count = slots // (ranks * pairs)
    down = lax.psum_scatter(
        jnp.dot(hidden_units, w_down, preferred_element_type=jnp.float32).astype(jnp.bfloat16),
        ("kv", "tp"),
        scatter_dimension=0,
        tiled=True,
    ).astype(jnp.float32)
    row_start = (kv_rank * pairs + tp_rank) * row_count
    kept = lax.dynamic_slice_in_dim(resid_f, row_start, row_count, 0)
    mixed = (kept + down).astype(jnp.bfloat16)
    return (mixed, new_pages[None])


def solution(mesh):
    return jax.shard_map(
        per_device,
        mesh=mesh,
        in_specs=(
            P("grp", "kv"),
            P("kv"),
            P(),
            P("kv", "tp"),
            P("tp", "kv", None),
            P(None, ("kv", "tp")),
            P(None, ("kv", "tp")),
            P(("kv", "tp"), None),
            P(("grp", "kv"), None, None, "tp"),
            P("grp", "kv", None, None, "tp"),
            P("grp", "kv"),
            P("grp", "kv"),
            P(),
            P(),
            P("grp", "kv"),
            P("grp", "kv"),
            P("grp", None, "tp"),
        ),
        out_specs=(P(("grp", "kv", "tp"), None), P("grp", "kv", None, None, "tp")),
        check_vma=False,
    )
```

profile of v0, /device:TPU:0, one launch (start us, length us, event | category | flops | bytes accessed | tf_op | source)
XLA Modules:
  0.0 407.0 jit_solution(611504076523170792)
XLA Ops:
  7.2 0.8 reshape.445
  7.9 0.8 reshape.450
  8.8 0.2 reduce_window_sum.17
  9.0 0.8 reshape.447
  9.9 0.1 select_reduce_fusion.3
  10.2 5.0 %gather_fusion.2 = bf16[16,2,128,512]{3,2,1,0:T(8,128)(2,1)} fusion(bf16[16,2,128,512]{3,2,1,0:T(8,128)(2,1)} %param.29, s32[1024]{0:T(1024)S(1)} %pad_clamp_fusion.2), kind=kCustom, calls=%fused_computation.clone | custom fusion | bytes 8388672 | tf_op jit(solution)/shard_map/jit(_take)/gather | solution.py:69
  15.2 4.7 %broadcast_select_fusion.2 = bf16[16,2,128,512]{3,2,1,0:T(8,128)(2,1)} fusion(bf16[16,2,128,512]{3,2,1,0:T(8,128)(2,1)} %gather_fusion.2, pred[16]{0:T(512)(128)(4,1)S(1)} %compare_and_fusion.2), kind=kLoop, calls=%fused_computation.18 | loop fusion | flops 2097152 | bytes 8388624 | tf_op jit(solution)/shard_map/jit(_take)/select_n | solution.py:69
  19.9 5.2 %all-to-all-start = ((bf16[16,2,128,512]{3,2,1,0:T(8,128)(2,1)}), bf16[16,2,128,512]{3,2,1,0:T(8,128)(2,1)}, u32[]{:S(2)}, u32[]{:S(2)}) async-start(bf16[16,2,128,512]{3,2,1,0:T(8,128)(2,1)} %broadcast_select_fusion.2), calls=%async_computation | async-start | bytes 8388608 | tf_op jit(solution)/shard_map/all_to_all | solution.py:70
  25.1 0.2 reduce_window_sum.18
  25.4 0.1 select_reduce_fusion.2
  25.9 47.8 %all-to-all-done = bf16[16,2,128,512]{3,2,1,0:T(8,128)(2,1)} async-done(((bf16[16,2,128,512]{3,2,1,0:T(8,128)(2,1)}), bf16[16,2,128,512]{3,2,1,0:T(8,128)(2,1)}, u32[]{:S(2)}, u32[]{:S(2)}) %all-to-all-start) | async-done | bytes 4194336 | tf_op jit(solution)/shard_map/all_to_all | solution.py:70
  73.7 5.0 %gather_fusion.3 = bf16[16,2,128,512]{3,2,1,0:T(8,128)(2,1)} fusion(bf16[16,2,128,512]{3,2,1,0:T(8,128)(2,1)} %all-to-all-done, s32[1024]{0:T(1024)S(1)} %pad_clamp_fusion.1), kind=kCustom, calls=%fused_computation.1.clone | custom fusion | bytes 8388672 | tf_op jit(solution)/shard_map/jit(_take)/gather | solution.py:85
  78.7 4.7 %broadcast_select_fusion.1 = bf16[16,2,128,512]{3,2,1,0:T(8,128)(2,1)} fusion(bf16[16,2,128,512]{3,2,1,0:T(8,128)(2,1)} %gather_fusion.3, pred[16]{0:T(512)(128)(4,1)S(1)} %compare_and_fusion.1), kind=kLoop, calls=%fused_computation.17 | loop fusion | flops 2097152 | bytes 8388624 | tf_op jit(solution)/shard_map/jit(_take)/select_n | solution.py:85
  83.4 5.2 %all-to-all-start.1 = ((bf16[16,2,128,512]{3,2,1,0:T(8,128)(2,1)}), bf16[16,2,128,512]{3,2,1,0:T(8,128)(2,1)}, u32[]{:S(2)}, u32[]{:S(2)}) async-start(bf16[16,2,128,512]{3,2,1,0:T(8,128)(2,1)} %broadcast_select_fusion.1), calls=%async_computation.1 | async-start | bytes 8388608 | tf_op jit(solution)/shard_map/all_to_all | solution.py:86
  88.7 4.0 fusion.7
  93.1 0.4 slice_convert_fusion
  93.5 0.2 copy.150
  93.7 0.2 copy.143
  93.9 0.7 copy.134
  94.6 9.3 %psum.22 = f32[128]{0:T(128)S(1)} all-reduce(f32[128]{0:T(128)S(1)} %multiply_reduce_fusion.1), channel_id=1, replica_groups=mesh['grp'=4,'kv'=4,'tp'=2] {'kv'}, use_global_device_ids=true, to_apply=%region_2.0 | all-reduce | flops 128 | bytes 1024 | tf_op jit(solution)/shard_map/psum | solution.py:161
  104.2 41.8 %all-reduce.3.cloned.1.call-done = f32[128,2048]{1,0:T(8,128)} async-done(((f32[128,2048]{1,0:T(8,128)}), f32[128,2048]{1,0:T(8,128)}) %all-reduce.3.cloned.1.call-update) | async-done | bytes 1048592 | tf_op jit(solution)/shard_map/psum | solution.py:161
  145.9 1.4 multiply_multiply_fusion
  147.3 0.7 reshape.444
  148.0 1.3 gather_fusion
  149.4 2.5 fusion.34
  151.9 29.4 %all-to-all-done.1 = bf16[16,2,128,512]{3,2,1,0:T(8,128)(2,1)} async-done(((bf16[16,2,128,512]{3,2,1,0:T(8,128)(2,1)}), bf16[16,2,128,512]{3,2,1,0:T(8,128)(2,1)}, u32[]{:S(2)}, u32[]{:S(2)}) %all-to-all-start.1) | async-done | bytes 4194336 | tf_op jit(solution)/shard_map/all_to_all | solution.py:86
  181.3 5.0 %gather_fusion.4 = bf16[16,2,128,512]{3,2,1,0:T(8,128)(2,1)} fusion(bf16[16,2,128,512]{3,2,1,0:T(8,128)(2,1)} %all-to-all-done.1, s32[1024]{0:T(1024)S(1)} %pad_clamp_fusion), kind=kCustom, calls=%fused_computation.2.clone | custom fusion | bytes 8388672 | tf_op jit(solution)/shard_map/jit(_take)/gather | solution.py:90
  186.3 2.8 broadcast_select_fusion
  189.1 2.9 pad_maximum_fusion
  192.0 3.5 copy.122
  195.5 4.2 %fusion.33 = (f32[24,4,4]{2,1,0:T(4,128)S(1)}, f32[24,4,4,128]{3,2,1,0:T(4,128)}) fusion(bf16[24,128,4,128]{1,3,2,0:T(8,128)(2,1)S(1)} %bitcast.91, f32[24,4,4,128]{3,2,1,0:T(4,128)} %gather_fusion, pred[24]{0:T(512)(128)(4,1)S(1)} %get-tuple-element.244, pred[24,128]{1,0:T(8,128)(4,1)S(1)} %iota_compare_fusion), kind=kOutput, calls=%fused_computation.125 | convolution fusion | flops 75644544 | bytes 3543576 | tf_op jit(solution)/shard_map/ikgd,itkd->ikgt/dot_general | solution.py:106
  200.0 0.2 copy.126
  200.2 1.8 exponential_select_fusion
  202.0 0.6 gather_fusion.1
  202.7 3.5 copy.130
  206.2 6.6 %fusion.13 = f32[24,4,4,128]{3,2,1,0:T(4,128)} fusion(bf16[24,128,4,128]{1,3,2,0:T(8,128)(2,1)S(1)} %bitcast.95, f32[24,4,4,128]{3,2,1,0:T(4,128)} %get-tuple-element.261, f32[24,4,4]{2,1,0:T(4,128)S(1)} %broadcast_select_fusion.3, pred[24,128]{1,0:T(8,128)(4,1)S(1)} %iota_compare_fusion), kind=kOutput, calls=%fused_computation.50 | convolution fusion | flops 75595776 | bytes 3543552 | tf_op jit(solution)/shard_map/ikgt,itkd->ikgd/dot_general | solution.py:120
  212.8 1.0 reshape.456
  214.0 1.0 copy.129
  215.0 1.7 convolution_add_fusion
  216.8 1.7 copy.135
  218.5 0.3 all-reduce.5.cloned.1.call-start
  218.8 6.7 %copy.138 = bf16[4096,512]{1,0:T(8,128)(2,1)} copy(bf16[4096,512]{0,1:T(8,128)(2,1)} %bitcast.92) | data formatting | bytes 8388608 | tf_op jit(solution)/shard_map/dot_general | solution.py:182
  225.5 0.4 fusion.14
  226.0 0.2 convolution_add_fusion.1
  226.2 8.0 %all-gather = f32[512,16]{0,1:T(8,128)S(1)} all-gather(f32[128,16]{0,1:T(8,128)S(1)} %convolution_add_fusion.1), channel_id=2, replica_groups=mesh['grp'=4,'kv'=4,'tp'=2] {'kv'}, dimensions={0}, use_global_device_ids=true | all-gather | bytes 40960 | tf_op jit(solution)/shard_map/all_gather | solution.py:16
  234.3 8.2 %all_gather.12 = f32[4,128,16]{1,2,0:T(8,128)S(1)} all-gather(f32[1,128,16]{1,2,0:T(8,128)S(1)} %bitcast.104), channel_id=1, replica_groups=mesh['grp'=4,'kv'=4,'tp'=2] {'kv'}, dimensions={0}, use_global_device_ids=true | all-gather | bytes 40960 | tf_op jit(solution)/shard_map/all_gather | solution.py:16
  242.5 26.1 %all-gather.3.cloned.1.call-done = f32[4,128,16,128]{3,2,1,0:T(8,128)} async-done(((f32[1,128,16,128]{3,2,1,0:T(8,128)}), f32[4,128,16,128]{3,2,1,0:T(8,128)}) %all-gather.3.cloned.1.call-update) | async-done | bytes 4194320 | tf_op jit(solution)/shard_map/all_gather | solution.py:16
  268.7 1.3 slice_bitcast_fusion
  270.0 6.5 %while.19 = (s32[]{:T(128)}, f32[128,16]{0,1:T(8,128)S(1)}, f32[128,16]{0,1:T(8,128)S(1)}, f32[128,16,128]{2,1,0:T(8,128)S(1)}, f32[4,128,16]{1,2,0:T(8,128)S(1)...) while((s32[]{:T(128)}, f32[128,16]{0,1:T(8,128)S(1)}, ...), condition=%wide.region_14.16_spmd, body=%wide.region_13.15_spmd.sunk | while | flops 798725 | bytes 3276955 | solution.py:21
  270.2 1.9 fusion.48
  272.4 1.9 fusion.48
  274.5 1.9 fusion.48
  276.5 0.4 copy.137
  276.9 3.7 add_convert_fusion
  280.7 0.7 copy.140
  281.3 1.4 copy.141
  282.7 56.8 %all-reduce.5.cloned.1.call-done = bf16[128,4096]{1,0:T(8,128)(2,1)} async-done(((bf16[128,4096]{1,0:T(8,128)(2,1)}), bf16[128,4096]{1,0:T(8,128)(2,1)}) %all-reduce.5.cloned.1.call-update) | async-done | bytes 1048592 | tf_op jit(solution)/shard_map/psum | solution.py:191
  339.6 1.5 multiply_reduce_fusion
  341.1 7.7 %convolution_multiply_fusion.1 = f32[128,1792]{1,0:T(8,128)S(1)} fusion(bf16[4096,1792]{1,0:T(8,128)(2,1)} %param.26, f32[4096]{0:T(1024)S(1)} %copy-done.7, bf16[128,4096]{1,0:T(8,128)(2,1)} %all-reduce.5.cloned.1.call-done, f32[128]{0:T(128)S(1)} %add_rsqrt_fusion), kind=kOutput, calls=%fused_computation.22 | convolution fusion | flops 1880850432 | bytes 16663040 | tf_op jit(solution)/shard_map/dot_general | solution.py:195
  348.8 14.8 %convolution_convert_fusion = bf16[128,4096]{1,0:T(8,128)(2,1)} fusion(bf16[1792,4096]{1,0:T(8,128)(2,1)} %param.28, bf16[4096,1792]{1,0:T(8,128)(2,1)} %param.27, f32[128,1792]{1,0:T(8,128)S(1)} %convolution_multiply_fusion.1, f32[4096]{0:T(1024)S(1)} %copy-done.7, bf16[128,4096]{1,0:T(8,128)(2,1)S(1)} %copy-done, f32[128]{0:T(128)S(1)} %add_rsqrt_fusion), kind=kOutput, calls=%fused_computation.15 | convolution fusion | flops 3761799168 | bytes 32391680 | tf_op jit(solution)/shard_map/dot_general | solution.py:200
  363.6 4.7 %fusion.46 = bf16[1,16,2,128,512]{4,3,2,1,0:T(8,128)(2,1)} fusion(bf16[16,2,128,512]{3,2,1,0:T(8,128)(2,1)} %gather_fusion.4, pred[16]{0:T(512)(128)(4,1)S(1)} %get-tuple-element.246), kind=kLoop, calls=%fused_computation.127 | loop fusion | flops 2097152 | bytes 8388624 | tf_op jit(solution)/shard_map/broadcast_in_dim | solution.py:208
  368.2 0.2 convert_element_type.86
  368.4 30.5 %reduce-scatter.2.cloned.1.call-done = bf16[16,4096]{1,0:T(8,128)(2,1)} async-done(((bf16[128,4096]{1,0:T(8,128)(2,1)}), bf16[16,4096]{1,0:T(8,128)(2,1)}) %reduce-scatter.2.cloned.1.call-update) | async-done | bytes 131088 | tf_op jit(solution)/shard_map/reduce_scatter | solution.py:199
  398.9 1.6 add_convert_fusion.1
  (92 shorter events, 3.2 us)
Async XLA Ops:
  19.9 53.8 %all-to-all-start = ((bf16[16,2,128,512]{3,2,1,0:T(8,128)(2,1)}), bf16[16,2,128,512]{3,2,1,0:T(8,128)(2,1)}, u32[]{:S(2)}, u32[]{:S(2)}) async-start(bf16[16,2,128,512]{3,2,1,0:T(8,128)(2,1)} %broadcast_select_fusion.2), calls=%async_computation | async-start | bytes 8388608 | tf_op jit(solution)/shard_map/all_to_all | solution.py:70
  83.4 5.3 %copy-start.1 = (bf16[128,1024]{1,0:T(8,128)(2,1)S(1)}, bf16[128,1024]{1,0:T(8,128)(2,1)}, u32[]{:S(2)}) copy-start(bf16[128,1024]{1,0:T(8,128)(2,1)} %param.21) | copy-start | bytes 786436
  83.4 5.3 %copy-start.8 = (f32[1024]{0:T(1024)S(1)}, f32[1024]{0:T(1024)}, u32[]{:S(2)}) copy-start(f32[1024]{0:T(1024)} %param.22) | copy-start | bytes 12292
  83.4 97.9 %all-to-all-start.1 = ((bf16[16,2,128,512]{3,2,1,0:T(8,128)(2,1)}), bf16[16,2,128,512]{3,2,1,0:T(8,128)(2,1)}, u32[]{:S(2)}, u32[]{:S(2)}) async-start(bf16[16,2,128,512]{3,2,1,0:T(8,128)(2,1)} %broadcast_select_fusion.1), calls=%async_computation.1 | async-start | bytes 8388608 | tf_op jit(solution)/shard_map/all_to_all | solution.py:86
  88.6 4.2 %copy-start.9 = (s32[1,16]{1,0:T(1,128)S(1)}, s32[1,16]{1,0:T(1,128)}, u32[]{:S(2)}) copy-start(s32[1,16]{1,0:T(1,128)} %param.35) | copy-start | bytes 196
  88.6 4.2 %copy-start.10 = (s32[1,8]{1,0:T(1,128)S(1)}, s32[1,8]{1,0:T(1,128)}, u32[]{:S(2)}) copy-start(s32[1,8]{1,0:T(1,128)} %param.31) | copy-start | bytes 100
  88.6 4.5 %copy-start.5 = (bf16[128,2,512]{2,1,0:T(2,128)(2,1)S(1)}, bf16[128,2,512]{2,1,0:T(2,128)(2,1)}, u32[]{:S(2)}) copy-start(bf16[128,2,512]{2,1,0:T(2,128)(2,1)} %param.37) | copy-start | bytes 786436
  88.6 4.9 %copy-start.11 = (s32[1,16]{1,0:T(1,128)S(1)}, s32[1,16]{1,0:T(1,128)}, u32[]{:S(2)}) copy-start(s32[1,16]{1,0:T(1,128)} %param.36) | copy-start | bytes 196
  88.6 4.9 %copy-start.12 = (s32[1,8]{1,0:T(1,128)S(1)}, s32[1,8]{1,0:T(1,128)}, u32[]{:S(2)}) copy-start(s32[1,8]{1,0:T(1,128)} %param.32) | copy-start | bytes 100
  88.6 57.3 %all-reduce.3.cloned.1.call-start = ((), (), s32[]{:S(2)}) async-start(), calls=%async_computation.3 | async-start | bytes 2097152 | tf_op jit(solution)/shard_map/psum | solution.py:161
  92.7 176.0 %all-gather.3.cloned.1.call-start = ((), (), s32[]{:S(2)}) async-start(), calls=%async_computation.4 | async-start | bytes 5242880 | tf_op jit(solution)/shard_map/all_gather | solution.py:16
  186.3 2.9 copy-start.2
  202.0 0.7 copy-start.3
  218.5 121.1 %all-reduce.5.cloned.1.call-start = ((), (), s32[]{:S(2)}) async-start(), calls=%async_computation.5 | async-start | bytes 2097152 | tf_op jit(solution)/shard_map/psum | solution.py:191
  218.8 6.7 %copy-start.6 = (f32[24,4,4,128]{3,2,1,0:T(4,128)S(1)}, f32[24,4,4,128]{3,2,1,0:T(4,128)}, u32[]{:S(2)}) copy-start(f32[24,4,4,128]{3,2,1,0:T(4,128)} %get-tuple-element.261) | copy-start | bytes 589828
  218.8 15.4 %copy-start.4 = (f32[128,4,4]{2,1,0:T(4,128)S(1)}, f32[128,4,4]{2,1,0:T(4,128)}, u32[]{:S(2)}) copy-start(f32[128,4,4]{2,1,0:T(4,128)} %copy-done.3) | copy-start | bytes 24580
  280.6 60.4 %copy-start.7 = (f32[4096]{0:T(1024)S(1)}, f32[4096]{0:T(1024)}, u32[]{:S(2)}) copy-start(f32[4096]{0:T(1024)} %param.23) | copy-start | bytes 49156
  282.7 116.2 %reduce-scatter.2.cloned.1.call-start = ((), (), s32[]{:S(2)}) async-start(), calls=%async_computation.6 | async-start | bytes 1179648 | tf_op jit(solution)/shard_map/reduce_scatter | solution.py:199
  341.1 7.7 %copy-start = (bf16[128,4096]{1,0:T(8,128)(2,1)S(1)}, bf16[128,4096]{1,0:T(8,128)(2,1)}, u32[]{:S(2)}) copy-start(bf16[128,4096]{1,0:T(8,128)(2,1)} %all-reduce.5.cloned.1.call-done) | copy-start | bytes 3145732
Sparse Core Ops, SparseCore 0:
  92.8 53.0 all-reduce.2
  218.6 50.0 all-gather.2
  282.8 56.6 all-reduce.4
  363.7 35.1 reduce-scatter.1
where the time goes:
time: 408 us; the launch traced here: 407 us
  waiting for transfers between devices  232 us (57%)
  matrix products  45.4 us (11%)
  local copies, waits for them, and re-layouts  43.9 us (11%)
  other arithmetic  34.8 us (9%)
  blocking collectives  25.5 us (6%)
  between operations  14.2 us (3%)
  starting transfers between devices  10.8 us (3%)
    psum x1, waiting for transfers between devices, per_device(): lax.psum(laid.reshape(slots, ranks * width_here).astype(jnp.bfloat16), ('...  56.8 us
    all_to_all x1, waiting for transfers between devices, move_pages(): lax.all_to_all(outgoing, 'kv', split_axis=0, concat_axis=0, tiled=True)  47.8 us
    psum x1, waiting for transfers between devices, per_device(): partial_query, squares = lax.psum((partial_query, squares), 'kv')  41.8 us
    reduce_scatter x1, waiting for transfers between devices, per_device(): lax.psum_scatter(jnp.dot(hidden_units, w_down, preferred_element_type=jnp...  30.5 us
    all_to_all x1, waiting for transfers between devices, move_pages(): lax.all_to_all(sorted_pages, 'grp', split_axis=0, concat_axis=0, tiled=True)  29.4 us
    all_gather x1, waiting for transfers between devices, combined_all(): gathered = jax.tree.map(lambda a: lax.all_gather(a, axis), part)  26.1 us
    all_gather x2, blocking collectives, combined_all(): gathered = jax.tree.map(lambda a: lax.all_gather(a, axis), part)  16.2 us
    dot_general x1, matrix products, per_device(): jnp.dot(hidden_units, w_down, preferred_element_type=jnp.float32)  14.8 us
  transfers between devices with their start and end apart: 6, of which 6 were waited for; matrix products, arithmetic and copies ran while one was open for 6% of the time, Pallas kernels for 0%

commit v1 on v0

--- a/solution.py
+++ b/solution.py
@@ -188,7 +188,9 @@
     laid = branch.reshape(slots, ranks, width_here)
     spot = (jnp.arange(ranks, dtype=jnp.int32) == kv_rank) & (tp_rank == 0)
     laid = laid + jnp.where(spot[None, :, None], features[:, None, :], 0.0)
-    resid = lax.psum(laid.reshape(slots, ranks * width_here).astype(jnp.bfloat16), ("kv", "tp"))
+    resid = lax.psum(
+        lax.psum(laid.reshape(slots, ranks * width_here).astype(jnp.bfloat16), "tp"), "kv"
+    )
     resid_f = resid.astype(jnp.float32)
     mlp_scale = lax.rsqrt(jnp.sum(resid_f * resid_f, axis=1) / D + norm_eps)
     normed_mlp = (resid_f * mlp_gain).astype(jnp.bfloat16)

time: 408 us -> 428 us (1.049)
  waiting for transfers between devices: 232 us -> 252 us
    psum x1 -> x2, waiting for transfers between devices: 56.8 us -> 76.1 us  [the longest x1 56.5 us: per_device(): lax.psum(lax.psum(laid.reshape(slots, ranks * width_here).astype(jnp.bflo...]
  transfers between devices with their start and end apart: 6 -> 7, of which waited for: 6 -> 7; matrix products, arithmetic and copies ran while one was open for 6% -> 6% of each run, Pallas kernels for 0% -> 0%
where the time goes in v1:
time: 428 us; the launch traced here: 427 us
  waiting for transfers between devices  252 us (59%)
  matrix products  45.4 us (11%)
  local copies, waits for them, and re-layouts  43.9 us (10%)
  other arithmetic  34.8 us (8%)
  blocking collectives  25.5 us (6%)
  between operations  14.2 us (3%)
  starting transfers between devices  10.8 us (3%)
    psum x1, waiting for transfers between devices, per_device(): lax.psum(lax.psum(laid.reshape(slots, ranks * width_here).astype(jnp.bflo...  56.5 us
    all_to_all x1, waiting for transfers between devices, move_pages(): lax.all_to_all(outgoing, 'kv', split_axis=0, concat_axis=0, tiled=True)  47.8 us
    psum x1, waiting for transfers between devices, per_device(): partial_query, squares = lax.psum((partial_query, squares), 'kv')  41.8 us
    reduce_scatter x1, waiting for transfers between devices, per_device(): lax.psum_scatter(jnp.dot(hidden_units, w_down, preferred_element_type=jnp...  31.2 us
    all_to_all x1, waiting for transfers between devices, move_pages(): lax.all_to_all(sorted_pages, 'grp', split_axis=0, concat_axis=0, tiled=True)  29.4 us
    all_gather x1, waiting for transfers between devices, combined_all(): gathered = jax.tree.map(lambda a: lax.all_gather(a, axis), part)  26.1 us
    psum x1, waiting for transfers between devices, per_device(): lax.psum(laid.reshape(slots, ranks * width_here).astype(jnp.bfloat16), 'tp')  19.5 us
    all_gather x2, blocking collectives, combined_all(): gathered = jax.tree.map(lambda a: lax.all_gather(a, axis), part)  16.2 us
  transfers between devices with their start and end apart: 7, of which 7 were waited for; matrix products, arithmetic and copies ran while one was open for 6% of the time, Pallas kernels for 0%

profile of v1, /device:TPU:0, one launch (start us, length us, event | category | flops | bytes accessed | tf_op | source)
XLA Modules:
  0.0 427.1 jit_solution(2824595694351304734)
XLA Ops:
  7.2 0.8 reshape.445
  7.9 0.8 reshape.450
  8.8 0.2 reduce_window_sum.17
  9.0 0.8 reshape.447
  9.9 0.1 select_reduce_fusion.3
  10.2 5.0 %gather_fusion.2 = bf16[16,2,128,512]{3,2,1,0:T(8,128)(2,1)} fusion(bf16[16,2,128,512]{3,2,1,0:T(8,128)(2,1)} %param.29, s32[1024]{0:T(1024)S(1)} %pad_clamp_fusion.2), kind=kCustom, calls=%fused_computation.clone | custom fusion | bytes 8388672 | tf_op jit(solution)/shard_map/jit(_take)/gather | solution.py:69
  15.2 4.7 %broadcast_select_fusion.2 = bf16[16,2,128,512]{3,2,1,0:T(8,128)(2,1)} fusion(bf16[16,2,128,512]{3,2,1,0:T(8,128)(2,1)} %gather_fusion.2, pred[16]{0:T(512)(128)(4,1)S(1)} %compare_and_fusion.2), kind=kLoop, calls=%fused_computation.18 | loop fusion | flops 2097152 | bytes 8388624 | tf_op jit(solution)/shard_map/jit(_take)/select_n | solution.py:69
  19.9 5.2 %all-to-all-start = ((bf16[16,2,128,512]{3,2,1,0:T(8,128)(2,1)}), bf16[16,2,128,512]{3,2,1,0:T(8,128)(2,1)}, u32[]{:S(2)}, u32[]{:S(2)}) async-start(bf16[16,2,128,512]{3,2,1,0:T(8,128)(2,1)} %broadcast_select_fusion.2), calls=%async_computation | async-start | bytes 8388608 | tf_op jit(solution)/shard_map/all_to_all | solution.py:70
  25.1 0.2 reduce_window_sum.18
  25.9 47.8 %all-to-all-done = bf16[16,2,128,512]{3,2,1,0:T(8,128)(2,1)} async-done(((bf16[16,2,128,512]{3,2,1,0:T(8,128)(2,1)}), bf16[16,2,128,512]{3,2,1,0:T(8,128)(2,1)}, u32[]{:S(2)}, u32[]{:S(2)}) %all-to-all-start) | async-done | bytes 4194336 | tf_op jit(solution)/shard_map/all_to_all | solution.py:70
  73.7 5.0 %gather_fusion.3 = bf16[16,2,128,512]{3,2,1,0:T(8,128)(2,1)} fusion(bf16[16,2,128,512]{3,2,1,0:T(8,128)(2,1)} %all-to-all-done, s32[1024]{0:T(1024)S(1)} %pad_clamp_fusion.1), kind=kCustom, calls=%fused_computation.1.clone | custom fusion | bytes 8388672 | tf_op jit(solution)/shard_map/jit(_take)/gather | solution.py:85
  78.7 4.7 %broadcast_select_fusion.1 = bf16[16,2,128,512]{3,2,1,0:T(8,128)(2,1)} fusion(bf16[16,2,128,512]{3,2,1,0:T(8,128)(2,1)} %gather_fusion.3, pred[16]{0:T(512)(128)(4,1)S(1)} %compare_and_fusion.1), kind=kLoop, calls=%fused_computation.17 | loop fusion | flops 2097152 | bytes 8388624 | tf_op jit(solution)/shard_map/jit(_take)/select_n | solution.py:85
  83.4 5.2 %all-to-all-start.1 = ((bf16[16,2,128,512]{3,2,1,0:T(8,128)(2,1)}), bf16[16,2,128,512]{3,2,1,0:T(8,128)(2,1)}, u32[]{:S(2)}, u32[]{:S(2)}) async-start(bf16[16,2,128,512]{3,2,1,0:T(8,128)(2,1)} %broadcast_select_fusion.1), calls=%async_computation.1 | async-start | bytes 8388608 | tf_op jit(solution)/shard_map/all_to_all | solution.py:86
  88.7 4.0 fusion.7
  93.1 0.4 slice_convert_fusion
  93.5 0.2 copy.150
  93.7 0.2 copy.143
  93.9 0.7 copy.134
  94.6 9.3 %psum.29 = f32[128]{0:T(128)S(1)} all-reduce(f32[128]{0:T(128)S(1)} %multiply_reduce_fusion.1), channel_id=1, replica_groups=mesh['grp'=4,'kv'=4,'tp'=2] {'kv'}, use_global_device_ids=true, to_apply=%region_2.0 | all-reduce | flops 128 | bytes 1024 | tf_op jit(solution)/shard_map/psum | solution.py:161
  104.2 41.8 %all-reduce.4.cloned.1.call-done = f32[128,2048]{1,0:T(8,128)} async-done(((f32[128,2048]{1,0:T(8,128)}), f32[128,2048]{1,0:T(8,128)}) %all-reduce.4.cloned.1.call-update) | async-done | bytes 1048592 | tf_op jit(solution)/shard_map/psum | solution.py:161
  145.9 1.4 multiply_multiply_fusion
  147.3 0.7 reshape.444
  148.0 1.3 gather_fusion
  149.4 2.5 fusion.34
  151.9 29.4 %all-to-all-done.1 = bf16[16,2,128,512]{3,2,1,0:T(8,128)(2,1)} async-done(((bf16[16,2,128,512]{3,2,1,0:T(8,128)(2,1)}), bf16[16,2,128,512]{3,2,1,0:T(8,128)(2,1)}, u32[]{:S(2)}, u32[]{:S(2)}) %all-to-all-start.1) | async-done | bytes 4194336 | tf_op jit(solution)/shard_map/all_to_all | solution.py:86
  181.3 5.0 %gather_fusion.4 = bf16[16,2,128,512]{3,2,1,0:T(8,128)(2,1)} fusion(bf16[16,2,128,512]{3,2,1,0:T(8,128)(2,1)} %all-to-all-done.1, s32[1024]{0:T(1024)S(1)} %pad_clamp_fusion), kind=kCustom, calls=%fused_computation.2.clone | custom fusion | bytes 8388672 | tf_op jit(solution)/shard_map/jit(_take)/gather | solution.py:90
  186.3 2.8 broadcast_select_fusion
  189.1 2.9 pad_maximum_fusion
  192.0 3.5 copy.122
  195.5 4.2 fusion.33
  200.0 0.2 copy.126
  200.2 1.8 exponential_select_fusion
  202.0 0.6 gather_fusion.1
  202.7 3.5 copy.130
  206.2 6.6 %fusion.13 = f32[24,4,4,128]{3,2,1,0:T(4,128)} fusion(bf16[24,128,4,128]{1,3,2,0:T(8,128)(2,1)S(1)} %bitcast.95, f32[24,4,4,128]{3,2,1,0:T(4,128)} %get-tuple-element.261, f32[24,4,4]{2,1,0:T(4,128)S(1)} %broadcast_select_fusion.3, pred[24,128]{1,0:T(8,128)(4,1)S(1)} %iota_compare_fusion), kind=kOutput, calls=%fused_computation.50 | convolution fusion | flops 75595776 | bytes 3543552 | tf_op jit(solution)/shard_map/ikgt,itkd->ikgd/dot_general | solution.py:120
  212.8 1.0 reshape.456
  214.0 1.0 copy.129
  215.0 1.7 convolution_add_fusion
  216.8 1.7 copy.135
  218.5 0.3 all-reduce.6.cloned.1.call-start
  218.8 6.7 %copy.138 = bf16[4096,512]{1,0:T(8,128)(2,1)} copy(bf16[4096,512]{0,1:T(8,128)(2,1)} %bitcast.92) | data formatting | bytes 8388608 | tf_op jit(solution)/shard_map/dot_general | solution.py:182
  225.5 0.4 fusion.14
  226.0 0.2 convolution_add_fusion.1
  226.2 8.0 %all-gather = f32[512,16]{0,1:T(8,128)S(1)} all-gather(f32[128,16]{0,1:T(8,128)S(1)} %convolution_add_fusion.1), channel_id=2, replica_groups=mesh['grp'=4,'kv'=4,'tp'=2] {'kv'}, dimensions={0}, use_global_device_ids=true | all-gather | bytes 40960 | tf_op jit(solution)/shard_map/all_gather | solution.py:16
  234.3 8.2 %all_gather.12 = f32[4,128,16]{1,2,0:T(8,128)S(1)} all-gather(f32[1,128,16]{1,2,0:T(8,128)S(1)} %bitcast.104), channel_id=1, replica_groups=mesh['grp'=4,'kv'=4,'tp'=2] {'kv'}, dimensions={0}, use_global_device_ids=true | all-gather | bytes 40960 | tf_op jit(solution)/shard_map/all_gather | solution.py:16
  242.5 26.1 %all-gather.3.cloned.1.call-done = f32[4,128,16,128]{3,2,1,0:T(8,128)} async-done(((f32[1,128,16,128]{3,2,1,0:T(8,128)}), f32[4,128,16,128]{3,2,1,0:T(8,128)}) %all-gather.3.cloned.1.call-update) | async-done | bytes 4194320 | tf_op jit(solution)/shard_map/all_gather | solution.py:16
  268.7 1.3 slice_bitcast_fusion
  270.0 6.5 %while.19 = (s32[]{:T(128)}, f32[128,16]{0,1:T(8,128)S(1)}, f32[128,16]{0,1:T(8,128)S(1)}, f32[128,16,128]{2,1,0:T(8,128)S(1)}, f32[4,128,16]{1,2,0:T(8,128)S(1)...) while((s32[]{:T(128)}, f32[128,16]{0,1:T(8,128)S(1)}, ...), condition=%wide.region_14.16_spmd, body=%wide.region_13.15_spmd.sunk | while | flops 798725 | bytes 3276955 | solution.py:21
  270.2 1.9 fusion.48
  272.4 1.9 fusion.48
  274.5 1.9 fusion.48
  276.5 0.4 copy.137
  276.9 3.7 add_convert_fusion
  280.7 0.7 copy.140
  281.3 1.4 copy.141
  282.7 19.5 %all-reduce.6.cloned.1.call-done = bf16[128,4096]{1,0:T(8,128)(2,1)} async-done(((bf16[128,4096]{1,0:T(8,128)(2,1)}), bf16[128,4096]{1,0:T(8,128)(2,1)}) %all-reduce.6.cloned.1.call-update) | async-done | bytes 1048592 | tf_op jit(solution)/shard_map/psum | solution.py:192
  302.4 56.5 %all-reduce.8.cloned.1.call-done = bf16[128,4096]{1,0:T(8,128)(2,1)} async-done(((bf16[128,4096]{1,0:T(8,128)(2,1)}), bf16[128,4096]{1,0:T(8,128)(2,1)}) %all-reduce.8.cloned.1.call-update) | async-done | bytes 1048592 | tf_op jit(solution)/shard_map/psum | solution.py:191
  358.9 1.5 multiply_reduce_fusion
  360.4 7.7 %convolution_multiply_fusion.1 = f32[128,1792]{1,0:T(8,128)S(1)} fusion(bf16[4096,1792]{1,0:T(8,128)(2,1)} %param.26, f32[4096]{0:T(1024)S(1)} %copy-done.7, bf16[128,4096]{1,0:T(8,128)(2,1)} %all-reduce.8.cloned.1.call-done, f32[128]{0:T(128)S(1)} %add_rsqrt_fusion), kind=kOutput, calls=%fused_computation.22 | convolution fusion | flops 1880850432 | bytes 16663040 | tf_op jit(solution)/shard_map/dot_general | solution.py:197
  368.1 14.8 %convolution_convert_fusion = bf16[128,4096]{1,0:T(8,128)(2,1)} fusion(bf16[1792,4096]{1,0:T(8,128)(2,1)} %param.28, bf16[4096,1792]{1,0:T(8,128)(2,1)} %param.27, f32[128,1792]{1,0:T(8,128)S(1)} %convolution_multiply_fusion.1, f32[4096]{0:T(1024)S(1)} %copy-done.7, bf16[128,4096]{1,0:T(8,128)(2,1)S(1)} %copy-done, f32[128]{0:T(128)S(1)} %add_rsqrt_fusion), kind=kOutput, calls=%fused_computation.15 | convolution fusion | flops 3761799168 | bytes 32391680 | tf_op jit(solution)/shard_map/dot_general | solution.py:202
  382.9 4.7 %fusion.46 = bf16[1,16,2,128,512]{4,3,2,1,0:T(8,128)(2,1)} fusion(bf16[16,2,128,512]{3,2,1,0:T(8,128)(2,1)} %gather_fusion.4, pred[16]{0:T(512)(128)(4,1)S(1)} %get-tuple-element.246), kind=kLoop, calls=%fused_computation.127 | loop fusion | flops 2097152 | bytes 8388624 | tf_op jit(solution)/shard_map/broadcast_in_dim | solution.py:210
  387.6 0.2 convert_element_type.86
  387.8 31.2 %reduce-scatter.2.cloned.1.call-done = bf16[16,4096]{1,0:T(8,128)(2,1)} async-done(((bf16[128,4096]{1,0:T(8,128)(2,1)}), bf16[16,4096]{1,0:T(8,128)(2,1)}) %reduce-scatter.2.cloned.1.call-update) | async-done | bytes 131088 | tf_op jit(solution)/shard_map/reduce_scatter | solution.py:201
  419.0 1.6 add_convert_fusion.1
  (95 shorter events, 3.4 us)
Async XLA Ops:
  19.9 53.8 %all-to-all-start = ((bf16[16,2,128,512]{3,2,1,0:T(8,128)(2,1)}), bf16[16,2,128,512]{3,2,1,0:T(8,128)(2,1)}, u32[]{:S(2)}, u32[]{:S(2)}) async-start(bf16[16,2,128,512]{3,2,1,0:T(8,128)(2,1)} %broadcast_select_fusion.2), calls=%async_computation | async-start | bytes 8388608 | tf_op jit(solution)/shard_map/all_to_all | solution.py:70
  83.4 5.3 %copy-start.1 = (bf16[128,1024]{1,0:T(8,128)(2,1)S(1)}, bf16[128,1024]{1,0:T(8,128)(2,1)}, u32[]{:S(2)}) copy-start(bf16[128,1024]{1,0:T(8,128)(2,1)} %param.21) | copy-start | bytes 786436
  83.4 5.3 %copy-start.8 = (f32[1024]{0:T(1024)S(1)}, f32[1024]{0:T(1024)}, u32[]{:S(2)}) copy-start(f32[1024]{0:T(1024)} %param.22) | copy-start | bytes 12292
  83.4 97.9 %all-to-all-start.1 = ((bf16[16,2,128,512]{3,2,1,0:T(8,128)(2,1)}), bf16[16,2,128,512]{3,2,1,0:T(8,128)(2,1)}, u32[]{:S(2)}, u32[]{:S(2)}) async-start(bf16[16,2,128,512]{3,2,1,0:T(8,128)(2,1)} %broadcast_select_fusion.1), calls=%async_computation.1 | async-start | bytes 8388608 | tf_op jit(solution)/shard_map/all_to_all | solution.py:86
  88.6 4.2 copy-start.9
  88.6 4.2 copy-start.10
  88.6 4.5 %copy-start.5 = (bf16[128,2,512]{2,1,0:T(2,128)(2,1)S(1)}, bf16[128,2,512]{2,1,0:T(2,128)(2,1)}, u32[]{:S(2)}) copy-start(bf16[128,2,512]{2,1,0:T(2,128)(2,1)} %param.37) | copy-start | bytes 786436
  88.6 4.9 %copy-start.11 = (s32[1,16]{1,0:T(1,128)S(1)}, s32[1,16]{1,0:T(1,128)}, u32[]{:S(2)}) copy-start(s32[1,16]{1,0:T(1,128)} %param.36) | copy-start | bytes 196
  88.6 4.9 %copy-start.12 = (s32[1,8]{1,0:T(1,128)S(1)}, s32[1,8]{1,0:T(1,128)}, u32[]{:S(2)}) copy-start(s32[1,8]{1,0:T(1,128)} %param.32) | copy-start | bytes 100
  88.6 57.3 %all-reduce.4.cloned.1.call-start = ((), (), s32[]{:S(2)}) async-start(), calls=%async_computation.3 | async-start | bytes 2097152 | tf_op jit(solution)/shard_map/psum | solution.py:161
  92.7 176.0 %all-gather.3.cloned.1.call-start = ((), (), s32[]{:S(2)}) async-start(), calls=%async_computation.4 | async-start | bytes 5242880 | tf_op jit(solution)/shard_map/all_gather | solution.py:16
  186.3 2.9 copy-start.2
  202.0 0.7 copy-start.3
  218.5 83.8 %all-reduce.6.cloned.1.call-start = ((), (), s32[]{:S(2)}) async-start(), calls=%async_computation.5 | async-start | bytes 2097152 | tf_op jit(solution)/shard_map/psum | solution.py:192
  218.8 6.7 %copy-start.6 = (f32[24,4,4,128]{3,2,1,0:T(4,128)S(1)}, f32[24,4,4,128]{3,2,1,0:T(4,128)}, u32[]{:S(2)}) copy-start(f32[24,4,4,128]{3,2,1,0:T(4,128)} %get-tuple-element.261) | copy-start | bytes 589828
  218.8 15.4 %copy-start.4 = (f32[128,4,4]{2,1,0:T(4,128)S(1)}, f32[128,4,4]{2,1,0:T(4,128)}, u32[]{:S(2)}) copy-start(f32[128,4,4]{2,1,0:T(4,128)} %copy-done.3) | copy-start | bytes 24580
  280.6 79.8 %copy-start.7 = (f32[4096]{0:T(1024)S(1)}, f32[4096]{0:T(1024)}, u32[]{:S(2)}) copy-start(f32[4096]{0:T(1024)} %param.23) | copy-start | bytes 49156
  282.7 76.2 %all-reduce.8.cloned.1.call-start = ((), (), s32[]{:S(2)}) async-start(), calls=%async_computation.6 | async-start | bytes 2097152 | tf_op jit(solution)/shard_map/psum | solution.py:191
  302.3 116.7 %reduce-scatter.2.cloned.1.call-start = ((), (), s32[]{:S(2)}) async-start(), calls=%async_computation.7 | async-start | bytes 1179648 | tf_op jit(solution)/shard_map/reduce_scatter | solution.py:201
  360.4 7.7 %copy-start = (bf16[128,4096]{1,0:T(8,128)(2,1)S(1)}, bf16[128,4096]{1,0:T(8,128)(2,1)}, u32[]{:S(2)}) copy-start(bf16[128,4096]{1,0:T(8,128)(2,1)} %all-reduce.8.cloned.1.call-done) | copy-start | bytes 3145732
Sparse Core Ops, SparseCore 0:
  92.8 53.0 all-reduce.3
  218.6 50.0 all-gather.2
  282.8 19.4 all-reduce.5
  305.2 53.6 all-reduce.7
  383.0 35.9 reduce-scatter.1
